TPU v7x, 32 devices: a whole 2x2x4 slice. The times are simulated.
32 devices in a mesh: seq: 8 (over z, y), head: 4 (over x, core).
Axes of the slice: x: 2, y: 2, z: 4, core: 2. Of those that a mesh axis runs over, the one named last changes fastest.
Arguments:
- query: bfloat16 [512, 2048], P('seq', 'head'), may hold values from -16 to 16
- key_states: bfloat16 [512, 2048], P('seq', 'head'), may hold values from -16 to 16
- value_states: bfloat16 [512, 2048], P('seq', 'head'), may hold values from -6 to 6
- doc_ids: int32 [512], P('seq'), may hold values from 0 to 3, never falling along the last dimension, each value on 1 to 256 neighbouring positions
- out_weight: bfloat16 [2048, 4096], P('head', 'seq'), may hold values from -0.1875 to 0.1875
- residual: bfloat16 [512, 4096], P('seq', 'head'), may hold values from -6 to 6
Outputs:
- mixed: bfloat16 [512, 4096], P('seq', 'head')
Inputs may be any that keep to these rules, and one draw needn't show every extreme that they name: doc_ids never fall along the sequence; every document has 1 to 256 positions, and one has exactly 256.
All inputs are finite; a program needn't handle non-finite values.
Results may differ from a plain program's by a relative error of at most 0.0055.
Values may be sent and summed in bfloat16 or wider, within the bound.
A program may use at most 64 MiB of HBM per device.

v0:
```python
import jax
import jax.numpy as jnp
from jax import lax
from jax.sharding import PartitionSpec as P

HEAD_DIM = 128


masked_score = -1e30


def to_heads(block):
    return block.reshape(block.shape[0], block.shape[1] // HEAD_DIM, HEAD_DIM)


def attend_block(state, queries, query_pos, query_docs, keys, values, key_pos, key_docs):
    run_max, run_sum, run_acc = state
    scores = jnp.einsum(
        "qhd,khd->hqk", queries, keys, preferred_element_type=jnp.float32
    ) * HEAD_DIM ** (-0.5)
    allowed = (key_pos[None, :] <= query_pos[:, None]) & (key_docs[None, :] == query_docs[:, None])
    scores = jnp.where(allowed[None], scores, masked_score)
    new_max = jnp.maximum(run_max, jnp.max(scores, axis=-1))
    weights = jnp.where(allowed[None], jnp.exp(scores - new_max[..., None]), 0.0)
    run_sum = jnp.sum(weights, axis=-1)
    run_acc = jnp.einsum(
        "hqk,khd->hqd", weights.astype(jnp.bfloat16), values, preferred_element_type=jnp.float32
    )
    return (new_max, run_sum, run_acc)


def shards(query, key_states, value_states, doc_ids, out_weight, residual):
    tok_rows = query.shape[0]
    heads = query.shape[1] // HEAD_DIM
    shard_index = lax.axis_index("seq")
    first_pos = shard_index * tok_rows
    groups = [(query, first_pos + jnp.arange(tok_rows, dtype=jnp.int32), doc_ids)]
    prepared = [(to_heads(block), block_pos, block_docs) for block, block_pos, block_docs in groups]
    initial = tuple(
        (
            (
                jnp.full((heads, block_pos.shape[0]), masked_score, jnp.float32),
                jnp.zeros((heads, block_pos.shape[0]), jnp.float32),
                jnp.zeros((heads, block_pos.shape[0], HEAD_DIM), jnp.float32),
            )
            for block, block_pos, block_docs in groups
        )
    )
    first_row = jnp.int32(0)
    keys = lax.all_gather(key_states, "seq", axis=0, tiled=True)
    values = lax.all_gather(value_states, "seq", axis=0, tiled=True)
    key_docs = lax.all_gather(doc_ids, "seq", axis=0, tiled=True)
    key_pos = jnp.arange(keys.shape[0], dtype=jnp.int32)
    key_heads = to_heads(keys)
    value_heads = to_heads(values)
    updated = []
    for member, state in zip(prepared, initial):
        queries, query_pos, query_docs = member

        def advance(inner, queries=queries, query_pos=query_pos, query_docs=query_docs):
            return attend_block(
                inner, queries, query_pos, query_docs, key_heads, value_heads, key_pos, key_docs
            )

        def unchanged(inner):
            return inner

        updated.append(lax.cond(first_row <= jnp.max(query_pos), advance, unchanged, state))
    finals = tuple(updated)
    outputs = []
    for run_max, run_sum, run_acc in finals:
        normed = run_acc / run_sum[..., None]
        outputs.append(
            jnp.transpose(normed, (1, 0, 2))
            .reshape(normed.shape[1], heads * HEAD_DIM)
            .astype(jnp.bfloat16)
        )
    attended = outputs[0]
    mapped = jnp.dot(
        attended,
        lax.all_gather(out_weight, "seq", axis=1, tiled=True),
        preferred_element_type=jnp.float32,
    )
    summed = lax.psum_scatter(mapped, "head", scatter_dimension=1, tiled=True)
    return (residual.astype(jnp.float32) + summed).astype(jnp.bfloat16)


def solution(mesh):
    placed = (
        P("seq", "head"),
        P("seq", "head"),
        P("seq", "head"),
        P("seq"),
        P("head", "seq"),
        P("seq", "head"),
    )
    return jax.shard_map(
        shards, mesh=mesh, in_specs=placed, out_specs=P("seq", "head"), check_vma=False
    )
```

profile of v0, /device:TPU:0, one launch (start us, length us, event | category | flops | bytes accessed | tf_op | source)
XLA Modules:
  0.0 137.0 jit_solution(2854361127337461728)
XLA Ops:
  6.5 0.0 all-gather.2.cloned.1.call-start
  6.5 0.7 all-gather.2.cloned.1.call-update
  7.3 0.0 reduce-scatter.2.cloned.1.call-start
  7.3 0.6 fusion.19
  8.6 1.3 dynamic-slice
  10.5 0.9 dynamic-update-slice
  11.3 13.2 %all-reduce = s32[512]{0:T(512)S(1)} all-reduce(s32[512]{0:T(512)S(1)} %dynamic-update-slice), channel_id=1, replica_groups=mesh['seq'=8,'head'=4] {'seq'}, use_global_device_ids=true, to_apply=%add | all-reduce | flops 512 | bytes 4096
  24.5 33.5 %all_gather.13 = bf16[512,512]{1,0:T(8,128)(2,1)S(1)} all-gather(bf16[64,512]{1,0:T(8,128)(2,1)} %param.9), channel_id=1, replica_groups=mesh['seq'=8,'head'=4] {'seq'}, dimensions={0}, use_global_device_ids=true | all-gather | bytes 589824 | tf_op jit(solution)/shard_map/all_gather | solution.py:50
  58.1 33.8 %all_gather.14 = bf16[512,512]{1,0:T(8,128)(2,1)S(1)} all-gather(bf16[64,512]{1,0:T(8,128)(2,1)} %param.10), channel_id=1, replica_groups=mesh['seq'=8,'head'=4] {'seq'}, dimensions={0}, use_global_device_ids=true | all-gather | bytes 589824 | tf_op jit(solution)/shard_map/all_gather | solution.py:51
  91.8 0.0 copy-start
  91.8 2.6 %conditional.1 = (f32[4,64]{1,0:T(4,128)S(1)}, f32[4,64,128]{2,1,0:T(8,128)S(1)}) conditional(s32[]{:T(128)} %convert_element_type.22, () %tuple.13, (s32[512]{0:T(512)S(1)}, s32[64]{0:T(128)S(1)}, s32[512]{0:T(512)S(1)}, s32[64]{0:T(128)}, bf16[64,512]{1,0:T(8,128)(2,1)}, /*index=5*/bf16[512,512]{1,0:T(8,128)(2,1)S(1)}, ...), branch_computations={%region_1.0_spmd, %region_2.5_spmd} | conditional | flops 68386560 | bytes 2959888 | solution.py:68
  91.8 0.8 compare_and_fusion
  92.6 1.2 fusion.20
  93.9 0.3 fusion.1
  94.2 0.2 fusion.7
  94.4 5.8 %all-gather.2.cloned.1.call-done = bf16[512,4096]{1,0:T(8,128)(2,1)} async-done(((bf16[512,512]{1,0:T(8,128)(2,1)}), bf16[512,4096]{1,0:T(8,128)(2,1)}) %all-gather.2.cloned.1.call-update) | async-done | bytes 4194320 | tf_op jit(solution)/shard_map/all_gather | solution.py:81
  100.2 4.1 %fusion.15 = f32[64,4096]{1,0:T(8,128)} fusion(bf16[512,4096]{1,0:T(8,128)(2,1)} %all-gather.2.cloned.1.call-done, f32[4,64,128]{2,1,0:T(8,128)S(1)} %get-tuple-element.31, f32[4,64]{1,0:T(4,128)S(1)} %get-tuple-element.32), kind=kOutput, calls=%fused_computation.20 | convolution fusion | flops 268500992 | bytes 5374976 | tf_op jit(solution)/shard_map/dot_general | solution.py:79
  104.2 0.0 reduce-scatter.2.cloned.1.call-update
  104.2 24.2 %reduce-scatter.2.cloned.1.call-done = f32[64,1024]{1,0:T(8,128)} async-done(((f32[64,4096]{1,0:T(8,128)}), f32[64,1024]{1,0:T(8,128)}) %reduce-scatter.2.cloned.1.call-update) | async-done | bytes 262160 | tf_op jit(solution)/shard_map/reduce_scatter | solution.py:84
  128.5 0.0 copy-done
  128.5 1.6 %add_convert_fusion = bf16[64,1024]{1,0:T(8,128)(2,1)} fusion(f32[64,1024]{1,0:T(8,128)} %reduce-scatter.2.cloned.1.call-done, bf16[64,1024]{1,0:T(8,128)(2,1)S(1)} %copy-done), kind=kLoop, calls=%fused_computation.18 | loop fusion | flops 196608 | bytes 524288 | tf_op jit(solution)/shard_map/convert_element_type | solution.py:85
  (4 shorter events, 0.0 us)
Async XLA Ops:
  6.5 93.6 %all-gather.2.cloned.1.call-start = ((), (), s32[]{:S(2)}) async-start(), calls=%async_computation.1 | async-start | bytes 4718592 | tf_op jit(solution)/shard_map/all_gather | solution.py:81
  7.3 121.2 %reduce-scatter.2.cloned.1.call-start = ((), (), s32[]{:S(2)}) async-start(), calls=%async_computation.2 | async-start | bytes 1310720 | tf_op jit(solution)/shard_map/reduce_scatter | solution.py:84
  91.8 36.7 %copy-start = (bf16[64,1024]{1,0:T(8,128)(2,1)S(1)}, bf16[64,1024]{1,0:T(8,128)(2,1)}, u32[]{:S(2)}) copy-start(bf16[64,1024]{1,0:T(8,128)(2,1)} %param.13) | copy-start | bytes 393220
Sparse Core Ops, SparseCore 0:
  9.4 90.7 all-gather.1
  104.4 24.0 reduce-scatter.1
where the time goes:
time: 137 us
  blocking collectives  80.5 us (59%)
  waiting for transfers between devices  30.7 us (22%)
  between operations  14.7 us (11%)
  matrix products  5.57 us (4%)
  other arithmetic  3.29 us (2%)
  local copies, waits for them, and re-layouts  2.12 us (2%)
    all_gather x1, blocking collectives, shards(): values = lax.all_gather(value_states, 'seq', axis=0, tiled=True)  33.8 us
    all_gather x1, blocking collectives, shards(): keys = lax.all_gather(key_states, 'seq', axis=0, tiled=True)  33.5 us
    reduce_scatter x1, waiting for transfers between devices, shards(): summed = lax.psum_scatter(mapped, 'head', scatter_dimension=1, tiled=True)  24.2 us
    unnamed x1, blocking collectives  13.2 us
    all_gather x1, waiting for transfers between devices, shards(): lax.all_gather(out_weight, 'seq', axis=1, tiled=True)  5.75 us
    dot_general x1, matrix products, shards(): jnp.dot(attended, lax.all_gather(out_weight, 'seq', axis=1, tiled=True),...  4.06 us
  transfers between devices with their start and end apart: 2, of which 2 were waited for; matrix products, arithmetic and copies ran while one was open for 4% of the time, Pallas kernels for 0%

commit v1 on v0

--- a/solution.py
+++ b/solution.py
@@ -1,6 +1,10 @@
+import functools
+
 import jax
 import jax.numpy as jnp
 from jax import lax
+from jax.experimental import pallas as pl
+from jax.experimental.pallas import tpu as pltpu
 from jax.sharding import PartitionSpec as P
 
 HEAD_DIM = 128
@@ -85,6 +89,297 @@
     return (residual.astype(jnp.float32) + summed).astype(jnp.bfloat16)
 
 
+MESH = pl.DeviceIdType.MESH
+
+
+def attention(queries, keys, values, doc_row, first_row, pos_rows):
+    rows, keep = queries.shape[0], keys.shape[0]
+    scores = lax.dot_general(
+        queries, keys, (((1,), (1,)), ((), ())), preferred_element_type=jnp.float32
+    ) * HEAD_DIM ** (-0.5)
+    row_pos = lax.broadcasted_iota(jnp.int32, (rows, keep), 0) + first_row
+    col_pos = lax.broadcasted_iota(jnp.int32, (rows, keep), 1)
+    docs = jnp.broadcast_to(doc_row, (rows, keep))
+    query_docs = jnp.sum(jnp.where(row_pos == col_pos, docs, 0), axis=1, keepdims=True)
+    allowed = (col_pos <= row_pos) & (docs == query_docs)
+    scores = jnp.where(allowed, scores, masked_score)
+    row_max = jnp.max(scores, axis=1, keepdims=True)
+    weights = jnp.where(allowed, jnp.exp(scores - row_max), 0.0)
+    row_sum = jnp.sum(weights, axis=1, keepdims=True)
+    product = jnp.dot(weights.astype(jnp.bfloat16), values, preferred_element_type=jnp.float32)
+    return (product / row_sum).astype(jnp.bfloat16)
+
+
+def fused_kernel(
+    n, nh, q_ref, k_ref, v_ref, doc_ref, w_ref, res_ref, out_ref,
+    qbuf, kbuf, vbuf, docbuf, att, wbuf, sendbuf, parts, resbuf,
+    q_send, q_recv, k_send, k_recv, v_send, v_recv, d_send, d_recv,
+    a_send, a_recv, f_send, f_recv, p_send, p_recv, w_sems, res_sem,
+):
+    me = lax.axis_index("seq")
+    head = lax.axis_index("head")
+    rows = k_ref.shape[0]
+    half = n // 2
+    mid = half * rows
+    plane, side = me // 2, me % 2
+    my_half = me // half
+    pair, core = head // 2, head % 2
+    partner = pair * 2 + (1 - core)
+    wrows, wcols = w_ref.shape[0], w_ref.shape[1] // 2
+
+    w_local = pltpu.make_async_copy(
+        w_ref.at[:, pl.ds(pl.multiple_of(core * wcols, wcols), wcols)],
+        wbuf.at[pl.ds(pl.multiple_of(core * wrows, wrows), wrows), :],
+        w_sems.at[0],
+    )
+    w_local.start()
+    res_copy = pltpu.make_async_copy(res_ref, resbuf, res_sem)
+    res_copy.start()
+
+    barrier = pltpu.get_barrier_semaphore()
+    for ds_ in range(n):
+        for dh in range(nh):
+            if ds_ == 0 and dh == 0:
+                continue
+            pl.semaphore_signal(
+                barrier, inc=1,
+                device_id=(lax.rem(me + ds_, n), lax.rem(head + dh, nh)),
+                device_id_type=MESH,
+            )
+    pl.semaphore_wait(barrier, n * nh - 1)
+
+    def block(ref, source):
+        return ref.at[pl.ds(pl.multiple_of(source * rows, rows), rows), :]
+
+    def lanes(ref, index):
+        return ref.at[:, pl.ds(pl.multiple_of(index * HEAD_DIM, HEAD_DIM), HEAD_DIM)]
+
+    def send_kv(kind, dst):
+        src, dest, ssem, rsem = kind
+        return pltpu.make_async_remote_copy(
+            src_ref=lanes(src, dst // 2), dst_ref=block(dest, me),
+            send_sem=ssem.at[dst], recv_sem=rsem.at[me],
+            device_id=(dst, head), device_id_type=MESH,
+        )
+
+    def local_kv(kind):
+        src, dest, ssem, rsem = kind
+        return pltpu.make_async_copy(lanes(src, plane), block(dest, me), rsem.at[me])
+
+    def send_q(dst):
+        return pltpu.make_async_remote_copy(
+            src_ref=lanes(q_ref, dst // 2), dst_ref=block(qbuf, me % half),
+            send_sem=q_send.at[dst], recv_sem=q_recv.at[me % half],
+            device_id=(dst, head), device_id_type=MESH,
+        )
+
+    def send_doc(dst):
+        return pltpu.make_async_remote_copy(
+            src_ref=doc_ref, dst_ref=docbuf.at[me],
+            send_sem=d_send.at[dst], recv_sem=d_recv.at[me],
+            device_id=(dst, head), device_id_type=MESH,
+        )
+
+    kinds = ((k_ref, kbuf, k_send, k_recv), (v_ref, vbuf, v_send, v_recv))
+
+    for off in range(1, n):
+        dst = lax.rem(me + off, n)
+
+        @pl.when((dst % 2 == 1) | (my_half == 0))
+        def _(dst=dst):
+            send_kv(kinds[0], dst).start()
+
+        @pl.when(dst % 2 == my_half)
+        def _(dst=dst):
+            send_q(dst).start()
+
+        send_doc(dst).start()
+
+        @pl.when((dst % 2 == 1) | (my_half == 0))
+        def _(dst=dst):
+            send_kv(kinds[1], dst).start()
+
+    w_remote = pltpu.make_async_remote_copy(
+        src_ref=w_ref.at[:, pl.ds(pl.multiple_of((1 - core) * wcols, wcols), wcols)],
+        dst_ref=wbuf.at[pl.ds(pl.multiple_of(core * wrows, wrows), wrows), :],
+        send_sem=w_sems.at[1], recv_sem=w_sems.at[2],
+        device_id=(me, partner), device_id_type=MESH,
+    )
+    w_remote.start()
+
+    @pl.when((side == 1) | (my_half == 0))
+    def _():
+        for kind in kinds:
+            local_kv(kind).start()
+
+    @pl.when(side == my_half)
+    def _():
+        pltpu.make_async_copy(
+            lanes(q_ref, plane), block(qbuf, me % half), q_recv.at[me % half]
+        ).start()
+
+    pltpu.make_async_copy(doc_ref, docbuf.at[me], d_recv.at[me]).start()
+
+    def arrived(ref, sem):
+        pltpu.make_async_copy(ref, ref, sem).wait()
+
+    for source in range(n):
+        arrived(docbuf.at[source], d_recv.at[source])
+    for source in range(half):
+        arrived(qbuf.at[pl.ds(source * rows, rows), :], q_recv.at[source])
+        for _, dest, _, rsem in kinds:
+            arrived(dest.at[pl.ds(source * rows, rows), :], rsem.at[source])
+
+    mine_rows = pl.ds(pl.multiple_of(side * mid, mid), mid)
+
+    def columns_of(c, index):
+        start = (c * half + index) * HEAD_DIM
+        return pl.ds(pl.multiple_of(start, HEAD_DIM), HEAD_DIM)
+
+    doc_row = jnp.concatenate([docbuf[source] for source in range(n)], axis=1)
+
+    @pl.when(side == 0)
+    def _():
+        att[mine_rows, columns_of(core, plane)] = attention(
+            qbuf[...], kbuf[:mid, :], vbuf[:mid, :], doc_row[:, :mid], 0, mid
+        )
+
+    @pl.when(side == 1)
+    def _():
+        for source in range(half, n):
+            for _, dest, _, rsem in kinds:
+                arrived(dest.at[pl.ds(source * rows, rows), :], rsem.at[source])
+        att[mine_rows, columns_of(core, plane)] = attention(
+            qbuf[...], kbuf[...], vbuf[...], doc_row, mid, mid
+        )
+
+    def att_block(c, source):
+        return att.at[
+            pl.ds(pl.multiple_of((source % 2) * mid, mid), mid), columns_of(c, source // 2)
+        ]
+
+    def att_send(dst):
+        return pltpu.make_async_remote_copy(
+            src_ref=att_block(core, me), dst_ref=att_block(core, me),
+            send_sem=a_send.at[dst], recv_sem=a_recv.at[me],
+            device_id=(dst, head), device_id_type=MESH,
+        )
+
+    def forward(source):
+        return pltpu.make_async_remote_copy(
+            src_ref=att_block(core, source), dst_ref=att_block(core, source),
+            send_sem=f_send.at[source], recv_sem=f_recv.at[source],
+            device_id=(me, partner), device_id_type=MESH,
+        )
+
+    order = [half, half + 1, half - 1, half + 2, half - 2, half + 3, half - 3]
+    for off in order:
+        att_send(lax.rem(me + off, n)).start()
+    forward(me).start()
+    for off in reversed(order):
+        source = lax.rem(me + off, n)
+        arrived(att_block(core, source), a_recv.at[source])
+        forward(source).start()
+
+    w_local.wait()
+    w_remote.wait()
+    for source in range(n):
+        arrived(att_block(1 - core, source), f_recv.at[source])
+
+    for piece in range(2):
+        span = slice(piece * mid, (piece + 1) * mid)
+        sendbuf[span, :] = jnp.dot(
+            att[span, :], wbuf[...], preferred_element_type=jnp.float32
+        ).astype(jnp.bfloat16)
+
+        for target in range(piece * half, (piece + 1) * half):
+            src = sendbuf.at[pl.ds(target * rows, rows), :]
+            slot = pair * 4 + side * 2 + core
+            own = (me == target) & (head == plane)
+
+            @pl.when(own)
+            def _(src=src, slot=slot):
+                pltpu.make_async_copy(src, parts.at[slot], p_recv.at[slot]).start()
+
+            @pl.when(jnp.logical_not(own))
+            def _(src=src, slot=slot, target=target):
+                pltpu.make_async_remote_copy(
+                    src_ref=src, dst_ref=parts.at[slot],
+                    send_sem=p_send.at[target], recv_sem=p_recv.at[slot],
+                    device_id=(target, plane), device_id_type=MESH,
+                ).start()
+
+    res_copy.wait()
+    for s in range(2):
+        for c in range(2):
+            a, b = s * 2 + c, 4 + s * 2 + c
+            arrived(parts.at[a], p_recv.at[a])
+            arrived(parts.at[b], p_recv.at[b])
+            start = (s * 2 + c) * wcols
+            cols = slice(start, start + wcols)
+            total = parts[a].astype(jnp.float32) + parts[b].astype(jnp.float32)
+            out_ref[:, cols] = (resbuf[:, cols].astype(jnp.float32) + total).astype(jnp.bfloat16)
+
+    for off in range(1, n):
+        dst = lax.rem(me + off, n)
+
+        @pl.when((dst % 2 == 1) | (my_half == 0))
+        def _(dst=dst):
+            for kind in kinds:
+                send_kv(kind, dst).wait_send()
+
+        @pl.when(dst % 2 == my_half)
+        def _(dst=dst):
+            send_q(dst).wait_send()
+
+        send_doc(dst).wait_send()
+        att_send(dst).wait_send()
+    for source in range(n):
+        forward(source).wait_send()
+    for target in range(n):
+        src = sendbuf.at[pl.ds(target * rows, rows), :]
+
+        @pl.when(jnp.logical_not((me == target) & (head == plane)))
+        def _(src=src, target=target):
+            pltpu.make_async_copy(src, src, p_send.at[target]).wait()
+
+
+def fused(n, nh, query, key_states, value_states, doc_ids, out_weight, residual):
+    rows, width = key_states.shape
+    wrows, wcols = out_weight.shape
+    seq = n * rows
+    dma = pltpu.SemaphoreType.DMA
+    vmem = pl.BlockSpec(memory_space=pltpu.VMEM)
+    any_ = pl.BlockSpec(memory_space=pl.ANY)
+    bf16 = jnp.bfloat16
+    return pl.pallas_call(
+        functools.partial(fused_kernel, n, nh),
+        out_shape=jax.ShapeDtypeStruct(residual.shape, residual.dtype),
+        in_specs=[vmem, vmem, vmem, vmem, any_, any_],
+        out_specs=vmem,
+        scratch_shapes=[
+            pltpu.VMEM((seq // 2, HEAD_DIM), bf16),
+            pltpu.VMEM((seq, HEAD_DIM), bf16),
+            pltpu.VMEM((seq, HEAD_DIM), bf16),
+            pltpu.VMEM((n, 1, rows), jnp.int32),
+            pltpu.VMEM((seq, 2 * width), bf16),
+            pltpu.VMEM((2 * wrows, wcols // 2), bf16),
+            pltpu.VMEM((seq, wcols // 2), bf16),
+            pltpu.VMEM((8, rows, wcols // 2), bf16),
+            pltpu.VMEM(residual.shape, bf16),
+            dma((n,)), dma((n // 2,)),
+            dma((n,)), dma((n,)),
+            dma((n,)), dma((n,)),
+            dma((n,)), dma((n,)),
+            dma((n,)), dma((n,)),
+            dma((n,)), dma((n,)),
+            dma((n,)), dma((8,)),
+            dma((3,)), dma,
+        ],
+        compiler_params=pltpu.CompilerParams(collective_id=0, has_side_effects=True),
+    )(query, key_states, value_states, doc_ids.reshape(1, rows), out_weight, residual)
+
+
 def solution(mesh):
     placed = (
         P("seq", "head"),
@@ -94,6 +389,20 @@
         P("head", "seq"),
         P("seq", "head"),
     )
+    n, nh = mesh.shape["seq"], mesh.shape["head"]
+
+    def body(query, key_states, value_states, doc_ids, out_weight, residual):
+        heads = query.shape[1] // HEAD_DIM
+        fits = (
+            n == 2 * heads
+            and n == 2 * nh
+            and nh % 2 == 0
+            and out_weight.shape[1] % 256 == 0
+            and query.shape[0] % 16 == 0
+        )
+        run = functools.partial(fused, n, nh) if fits else shards
+        return run(query, key_states, value_states, doc_ids, out_weight, residual)
+
     return jax.shard_map(
-        shards, mesh=mesh, in_specs=placed, out_specs=P("seq", "head"), check_vma=False
-    )
+        body, mesh=mesh, in_specs=placed, out_specs=P("seq", "head"), check_vma=False
+    )

time: 137 us -> 40.3 us (0.29)
  blocking collectives: 80.5 us -> 0 us
  Pallas kernels: 0 us -> 37.9 us
  waiting for transfers between devices: 30.7 us -> 0 us
  between operations: 14.7 us -> 0.01 us
  matrix products: 5.57 us -> 0 us
  other arithmetic: 3.29 us -> 0 us
    all_gather x2 -> x0, blocking collectives: 67.3 us -> none  [the longest x1 33.8 us: shards(): values = lax.all_gather(value_states, 'seq', axis=0, tiled=True)]
    pallas_call x0 -> x1, Pallas kernels: none -> 37.9 us  [fused(): pl.pallas_call(functools.partial(fused_kernel, n, nh), out_shape=jax.Shap...]
    reduce_scatter x1 -> x0, waiting for transfers between devices: 24.2 us -> none  [shards(): summed = lax.psum_scatter(mapped, 'head', scatter_dimension=1, tiled=True)]
    unnamed x1 -> x0, blocking collectives: 13.2 us -> none
    all_gather x1 -> x0, waiting for transfers between devices: 5.75 us -> none  [shards(): lax.all_gather(out_weight, 'seq', axis=1, tiled=True)]
    dot_general x3 -> x0, matrix products: 5.57 us -> none  [the longest x1 4.06 us: shards(): jnp.dot(attended, lax.all_gather(out_weight, 'seq', axis=1, tiled=True),...]
    convert_element_type x1 -> x0, other arithmetic: 1.63 us -> none  [shards(): return (residual.astype(jnp.float32) + summed).astype(jnp.bfloat16)]
  transfers between devices with their start and end apart: 2 -> 0, of which waited for: 2 -> 0; matrix products, arithmetic and copies ran while one was open for 4% -> 0% of each run, Pallas kernels for 0% -> 0%
where the time goes in v1:
time: 40.3 us; the launch traced here: 39.5 us
  Pallas kernels  37.9 us (94%)
  local copies, waits for them, and re-layouts  1.57 us (4%)
    pallas_call x1, Pallas kernels, fused(): pl.pallas_call(functools.partial(fused_kernel, n, nh), out_shape=jax.Shap...  37.9 us
    unnamed x1, local copies, waits for them, and re-layouts  1.57 us

profile of v1, /device:TPU:0, one launch (start us, length us, event | category | flops | bytes accessed | tf_op | source)
XLA Modules:
  0.0 39.5 jit_solution(17481597150437407013)
XLA Ops:
  0.0 37.9 %shard_map.64 = bf16[64,1024]{1,0:T(8,128)(2,1)} custom-call(bf16[64,512]{1,0:T(8,128)(2,1)} %q_ref.1, bf16[64,512]{1,0:T(8,128)(2,1)} %k_ref.1, bf16[64,512]{1,0:T(8,128)(2,1)} %v_ref.1, s32[1,64]{1,0:T(1,128)} %bitcast.1, bf16[512,512]{1,0:T(8,128)(2,1)} %w_ref.1, bf16[64,1024]{1,0:T(8,128)(2,1)} %res_ref.1), custom_call_target="tpu_custom_call" | custom-call | tf_op jit(solution)/shard_map/pallas_call | solution.py:355
  37.9 1.6 %copy.8 = bf16[64,1024]{1,0:T(8,128)(2,1)} copy(bf16[64,1024]{1,0:T(8,128)(2,1)} %shard_map.64) | data formatting | bytes 262144

commit v2 on v1

--- a/solution.py
+++ b/solution.py
@@ -90,6 +90,9 @@
 
 
 MESH = pl.DeviceIdType.MESH
+
+
+CHUNKS = 2
 
 
 def attention(queries, keys, values, doc_row, first_row, pos_rows):
@@ -114,7 +117,7 @@
     n, nh, q_ref, k_ref, v_ref, doc_ref, w_ref, res_ref, out_ref,
     qbuf, kbuf, vbuf, docbuf, att, wbuf, sendbuf, parts, resbuf,
     q_send, q_recv, k_send, k_recv, v_send, v_recv, d_send, d_recv,
-    a_send, a_recv, f_send, f_recv, p_send, p_recv, w_sems, res_sem,
+    z_send, z_recv, f_send, f_recv, p_send, p_recv, w_sems, w_recv, res_sem,
 ):
     me = lax.axis_index("seq")
     head = lax.axis_index("head")
@@ -125,14 +128,9 @@
     my_half = me // half
     pair, core = head // 2, head % 2
     partner = pair * 2 + (1 - core)
-    wrows, wcols = w_ref.shape[0], w_ref.shape[1] // 2
-
-    w_local = pltpu.make_async_copy(
-        w_ref.at[:, pl.ds(pl.multiple_of(core * wcols, wcols), wcols)],
-        wbuf.at[pl.ds(pl.multiple_of(core * wrows, wrows), wrows), :],
-        w_sems.at[0],
-    )
-    w_local.start()
+    wrows, wcols = w_ref.shape
+    w_slot = wbuf.at[pl.ds(pl.multiple_of(core * wrows, wrows), wrows), :]
+
     res_copy = pltpu.make_async_copy(res_ref, resbuf, res_sem)
     res_copy.start()
 
@@ -199,13 +197,23 @@
         def _(dst=dst):
             send_kv(kinds[1], dst).start()
 
-    w_remote = pltpu.make_async_remote_copy(
-        src_ref=w_ref.at[:, pl.ds(pl.multiple_of((1 - core) * wcols, wcols), wcols)],
-        dst_ref=wbuf.at[pl.ds(pl.multiple_of(core * wrows, wrows), wrows), :],
-        send_sem=w_sems.at[1], recv_sem=w_sems.at[2],
-        device_id=(me, partner), device_id_type=MESH,
-    )
-    w_remote.start()
+    def w_send(to, sem):
+        return pltpu.make_async_remote_copy(
+            src_ref=w_ref, dst_ref=w_slot, send_sem=w_sems.at[sem], recv_sem=w_recv.at[core],
+            device_id=to, device_id_type=MESH,
+        )
+
+    w_across = w_send((2 * plane + 1 - side, pair * 2 + side), 0)
+    w_beside = w_send((me, partner), 1)
+    w_across.start()
+
+    @pl.when(core == side)
+    def _():
+        pltpu.make_async_copy(w_ref, w_slot, w_recv.at[core]).start()
+
+    @pl.when(core != side)
+    def _():
+        w_beside.start()
 
     @pl.when((side == 1) | (my_half == 0))
     def _():
@@ -230,17 +238,11 @@
         for _, dest, _, rsem in kinds:
             arrived(dest.at[pl.ds(source * rows, rows), :], rsem.at[source])
 
-    mine_rows = pl.ds(pl.multiple_of(side * mid, mid), mid)
-
-    def columns_of(c, index):
-        start = (c * half + index) * HEAD_DIM
-        return pl.ds(pl.multiple_of(start, HEAD_DIM), HEAD_DIM)
-
     doc_row = jnp.concatenate([docbuf[source] for source in range(n)], axis=1)
 
     @pl.when(side == 0)
     def _():
-        att[mine_rows, columns_of(core, plane)] = attention(
+        att[core * half + plane] = attention(
             qbuf[...], kbuf[:mid, :], vbuf[:mid, :], doc_row[:, :mid], 0, mid
         )
 
@@ -249,76 +251,83 @@
         for source in range(half, n):
             for _, dest, _, rsem in kinds:
                 arrived(dest.at[pl.ds(source * rows, rows), :], rsem.at[source])
-        att[mine_rows, columns_of(core, plane)] = attention(
+        att[core * half + plane] = attention(
             qbuf[...], kbuf[...], vbuf[...], doc_row, mid, mid
         )
 
-    def att_block(c, source):
+    chunk = mid // CHUNKS
+
+    def att_chunk(c, source, part):
+        start = part * chunk
         return att.at[
-            pl.ds(pl.multiple_of((source % 2) * mid, mid), mid), columns_of(c, source // 2)
+            c * half + source // 2, pl.ds(pl.multiple_of(start, chunk), chunk), :
         ]
 
-    def att_send(dst):
+    def att_copy(source, part, send, recv, to):
+        ref = att_chunk(core, source, part)
         return pltpu.make_async_remote_copy(
-            src_ref=att_block(core, me), dst_ref=att_block(core, me),
-            send_sem=a_send.at[dst], recv_sem=a_recv.at[me],
-            device_id=(dst, head), device_id_type=MESH,
-        )
-
-    def forward(source):
-        return pltpu.make_async_remote_copy(
-            src_ref=att_block(core, source), dst_ref=att_block(core, source),
-            send_sem=f_send.at[source], recv_sem=f_recv.at[source],
-            device_id=(me, partner), device_id_type=MESH,
-        )
-
-    order = [half, half + 1, half - 1, half + 2, half - 2, half + 3, half - 3]
-    for off in order:
-        att_send(lax.rem(me + off, n)).start()
-    forward(me).start()
-    for off in reversed(order):
-        source = lax.rem(me + off, n)
-        arrived(att_block(core, source), a_recv.at[source])
-        forward(source).start()
-
-    w_local.wait()
-    w_remote.wait()
-    for source in range(n):
-        arrived(att_block(1 - core, source), f_recv.at[source])
-
-    for piece in range(2):
-        span = slice(piece * mid, (piece + 1) * mid)
-        sendbuf[span, :] = jnp.dot(
-            att[span, :], wbuf[...], preferred_element_type=jnp.float32
-        ).astype(jnp.bfloat16)
-
-        for target in range(piece * half, (piece + 1) * half):
-            src = sendbuf.at[pl.ds(target * rows, rows), :]
-            slot = pair * 4 + side * 2 + core
-            own = (me == target) & (head == plane)
-
-            @pl.when(own)
-            def _(src=src, slot=slot):
-                pltpu.make_async_copy(src, parts.at[slot], p_recv.at[slot]).start()
-
-            @pl.when(jnp.logical_not(own))
-            def _(src=src, slot=slot, target=target):
-                pltpu.make_async_remote_copy(
-                    src_ref=src, dst_ref=parts.at[slot],
-                    send_sem=p_send.at[target], recv_sem=p_recv.at[slot],
-                    device_id=(target, plane), device_id_type=MESH,
-                ).start()
+            src_ref=ref, dst_ref=ref, send_sem=send, recv_sem=recv,
+            device_id=to, device_id_type=MESH,
+        )
+
+    def along(dz, part):
+        return att_copy(
+            me, part, z_send.at[dz, part], z_recv.at[plane, part], (2 * dz + side, head)
+        )
+
+    def forward(source, part):
+        return att_copy(
+            source, part, f_send.at[source // 2, part], f_recv.at[source // 2, part], (me, partner)
+        )
+
+    offsets = list(range(1, half))
+    near_first = sorted(offsets, key=lambda off: min(off, half - off))
+    for off in reversed(near_first):
+        for part in range(CHUNKS):
+            along(lax.rem(plane + off, half), part).start()
+    for part in range(CHUNKS):
+        forward(me, part).start()
+
+    for off in near_first:
+        sz = lax.rem(plane + off, half)
+        for part in range(CHUNKS):
+            arrived(att_chunk(core, 2 * sz + side, part), z_recv.at[sz, part])
+            forward(2 * sz + side, part).start()
+
+    for slot in range(2):
+        arrived(wbuf.at[pl.ds(slot * wrows, wrows), :], w_recv.at[slot])
+    for sz in range(half):
+        for part in range(CHUNKS):
+            arrived(att_chunk(1 - core, 2 * sz + side, part), f_recv.at[sz, part])
+    attended = jnp.concatenate([att[index] for index in range(n)], axis=1)
+    sendbuf[...] = jnp.dot(
+        attended, wbuf[...], preferred_element_type=jnp.float32
+    ).astype(jnp.bfloat16)
+    slot = pair * 2 + core
+    for index in range(half):
+        target = side * half + index
+        src = sendbuf.at[pl.ds(index * rows, rows), :]
+        own = (me == target) & (head == plane)
+
+        @pl.when(own)
+        def _(src=src):
+            pltpu.make_async_copy(src, parts.at[slot], p_recv.at[slot]).start()
+
+        @pl.when(jnp.logical_not(own))
+        def _(src=src, target=target, index=index):
+            pltpu.make_async_remote_copy(
+                src_ref=src, dst_ref=parts.at[slot],
+                send_sem=p_send.at[index], recv_sem=p_recv.at[slot],
+                device_id=(target, plane), device_id_type=MESH,
+            ).start()
 
     res_copy.wait()
-    for s in range(2):
-        for c in range(2):
-            a, b = s * 2 + c, 4 + s * 2 + c
-            arrived(parts.at[a], p_recv.at[a])
-            arrived(parts.at[b], p_recv.at[b])
-            start = (s * 2 + c) * wcols
-            cols = slice(start, start + wcols)
-            total = parts[a].astype(jnp.float32) + parts[b].astype(jnp.float32)
-            out_ref[:, cols] = (resbuf[:, cols].astype(jnp.float32) + total).astype(jnp.bfloat16)
+    for c in range(2):
+        for p in range(2):
+            arrived(parts.at[2 * p + c], p_recv.at[2 * p + c])
+        cols = slice(c * wcols, (c + 1) * wcols)
+        total = parts[c].astype(jnp.float32) + parts[2 + c].astype(jnp.float32)
+        out_ref[:, cols] = (resbuf[:, cols].astype(jnp.float32) + total).astype(jnp.bfloat16)
 
     for off in range(1, n):
         dst = lax.rem(me + off, n)
@@ -333,15 +342,23 @@
             send_q(dst).wait_send()
 
         send_doc(dst).wait_send()
-        att_send(dst).wait_send()
-    for source in range(n):
-        forward(source).wait_send()
-    for target in range(n):
-        src = sendbuf.at[pl.ds(target * rows, rows), :]
-
-        @pl.when(jnp.logical_not((me == target) & (head == plane)))
-        def _(src=src, target=target):
-            pltpu.make_async_copy(src, src, p_send.at[target]).wait()
+    for part in range(CHUNKS):
+        for off in near_first:
+            along(lax.rem(plane + off, half), part).wait_send()
+        for sz in range(half):
+            forward(2 * sz + side, part).wait_send()
+    w_across.wait_send()
+
+    @pl.when(core != side)
+    def _():
+        w_beside.wait_send()
+
+    for index in range(half):
+        src = sendbuf.at[pl.ds(index * rows, rows), :]
+
+        @pl.when(jnp.logical_not((me == side * half + index) & (head == plane)))
+        def _(src=src, index=index):
+            pltpu.make_async_copy(src, src, p_send.at[index]).wait()
 
 
 def fused(n, nh, query, key_states, value_states, doc_ids, out_weight, residual):
@@ -362,19 +379,19 @@
             pltpu.VMEM((seq, HEAD_DIM), bf16),
             pltpu.VMEM((seq, HEAD_DIM), bf16),
             pltpu.VMEM((n, 1, rows), jnp.int32),
-            pltpu.VMEM((seq, 2 * width), bf16),
-            pltpu.VMEM((2 * wrows, wcols // 2), bf16),
-            pltpu.VMEM((seq, wcols // 2), bf16),
-            pltpu.VMEM((8, rows, wcols // 2), bf16),
+            pltpu.VMEM((n, seq // 2, HEAD_DIM), bf16),
+            pltpu.VMEM((2 * wrows, wcols), bf16),
+            pltpu.VMEM((seq // 2, wcols), bf16),
+            pltpu.VMEM((4, rows, wcols), bf16),
             pltpu.VMEM(residual.shape, bf16),
             dma((n,)), dma((n // 2,)),
             dma((n,)), dma((n,)),
             dma((n,)), dma((n,)),
             dma((n,)), dma((n,)),
-            dma((n,)), dma((n,)),
-            dma((n,)), dma((n,)),
-            dma((n,)), dma((8,)),
-            dma((3,)), dma,
+            dma((n // 2, CHUNKS)), dma((n // 2, CHUNKS)),
+            dma((n // 2, CHUNKS)), dma((n // 2, CHUNKS)),
+            dma((n // 2,)), dma((4,)),
+            dma((2,)), dma((2,)), dma,
         ],
         compiler_params=pltpu.CompilerParams(collective_id=0, has_side_effects=True),
     )(query, key_states, value_states, doc_ids.reshape(1, rows), out_weight, residual)

time: 40.3 us -> 40 us (level)
  the two profiles are of different devices: /device:TPU:0 before, /device:TPU:25 now
where the time goes in v2:
time: 40 us; the launch traced here: 39.9 us
  Pallas kernels  38.3 us (96%)
  local copies, waits for them, and re-layouts  1.57 us (4%)
    pallas_call x1, Pallas kernels, fused(): pl.pallas_call(functools.partial(fused_kernel, n, nh), out_shape=jax.Shap...  38.3 us
    unnamed x1, local copies, waits for them, and re-layouts  1.57 us

profile of v2, /device:TPU:25, one launch (start us, length us, event | category | flops | bytes accessed | tf_op | source)
XLA Modules:
  0.0 39.9 jit_solution(5225403582056419137)
XLA Ops:
  0.0 38.3 %shard_map.64 = bf16[64,1024]{1,0:T(8,128)(2,1)} custom-call(bf16[64,512]{1,0:T(8,128)(2,1)} %q_ref.1, bf16[64,512]{1,0:T(8,128)(2,1)} %k_ref.1, bf16[64,512]{1,0:T(8,128)(2,1)} %v_ref.1, s32[1,64]{1,0:T(1,128)} %bitcast.1, bf16[512,512]{1,0:T(8,128)(2,1)} %w_ref.1, bf16[64,1024]{1,0:T(8,128)(2,1)} %res_ref.1), custom_call_target="tpu_custom_call" | custom-call | tf_op jit(solution)/shard_map/pallas_call | solution.py:372
  38.3 1.6 %copy.8 = bf16[64,1024]{1,0:T(8,128)(2,1)} copy(bf16[64,1024]{1,0:T(8,128)(2,1)} %shard_map.64) | data formatting | bytes 262144
